TPU v7x, 32 devices: a whole 2x2x4 slice. The times are simulated.
32 devices in a mesh: gx: 4 (over z), gy: 4 (over y, x), gz: 2 (over core).
Axes of the slice: x: 2, y: 2, z: 4, core: 2. Of those that a mesh axis runs over, the one named last changes fastest.
Arguments:
- velocity: float32 [3, 32, 64, 256], P(None, 'gx', 'gy', 'gz'), may hold values from -6 to 6
- density: float32 [32, 64, 256], P('gx', 'gy', 'gz'), may hold values from 0 to 2
- offsets: int32 [3, 32, 64, 256], P(None, 'gx', 'gy', 'gz'), may hold values from -4 to 3
- eighths: int32 [3, 32, 64, 256], P(None, 'gx', 'gy', 'gz'), may hold values from 0 to 7
Outputs:
- new_velocity: float32 [3, 32, 64, 256], P(None, 'gx', 'gy', 'gz')
- new_density: float32 [32, 64, 256], P('gx', 'gy', 'gz')
- pressure: float32 [32, 64, 256], P('gx', 'gy', 'gz')
All inputs are finite; a program needn't handle non-finite values.
Results may differ from a plain program's by a relative error of at most 0.00002.
Values sent between devices are 32-bit elements; how exact they have to be, the bound alone decides.
A program may use at most 64 MiB of HBM per device.

v0:
```python
import jax
import jax.numpy as jnp
from jax import lax
from jax.sharding import PartitionSpec as P

RELAX_WEIGHT = 6.0 / 7.0


def padded_2(block, sides, width):
    for axis, dim in sides:
        count = lax.axis_size(axis)
        forward = [(i, i + 1) for i in range(count - 1)]
        backward = [(target, source) for source, target in forward]
        low = lax.ppermute(
            lax.slice_in_dim(block, block.shape[dim] - width, None, axis=dim), axis, forward
        )
        high = lax.ppermute(lax.slice_in_dim(block, 0, width, axis=dim), axis, backward)
        block = jnp.concatenate([low, block, high], axis=dim)
    return block


def neighbours(padded):
    summed = padded[2:, 1:-1, 1:-1] + padded[:-2, 1:-1, 1:-1]
    summed = summed + padded[1:-1, 2:, 1:-1] + padded[1:-1, :-2, 1:-1]
    summed = summed + padded[1:-1, 1:-1, 2:] + padded[1:-1, 1:-1, :-2]
    return summed


def operate(padded):
    return 6.0 * padded[1:-1, 1:-1, 1:-1] - neighbours(padded)


def axis_weights(offset_axis, fraction_axis):
    levels = lax.broadcasted_iota(jnp.int32, (9, 1, 1, 1), 0) - 4
    lower = jnp.where(offset_axis[None] == levels, 1.0 - fraction_axis[None], jnp.float32(0.0))
    upper = jnp.where(offset_axis[None] == levels - 1, fraction_axis[None], jnp.float32(0.0))
    return lower + upper


def advect_block(padded, offsets, eighths):
    field_count = padded.shape[0]
    box_shape = offsets.shape[1:]
    fraction = eighths.astype(jnp.float32) / 8.0
    weight_x = axis_weights(offsets[0], fraction[0])
    weight_y = axis_weights(offsets[1], fraction[1])
    weight_z = axis_weights(offsets[2], fraction[2])

    def one_plane(step_x, summed):
        slab = lax.dynamic_slice_in_dim(padded, step_x, box_shape[0], 1)
        plane_weight = lax.dynamic_index_in_dim(weight_x, step_x, 0, keepdims=False)
        for step_y in range(9):
            window = slab[:, :, step_y : step_y + box_shape[1], :]
            along_z = jnp.zeros((field_count,) + box_shape, jnp.float32)
            for step_z in range(9):
                along_z = (
                    along_z
                    + weight_z[step_z][None] * window[:, :, :, step_z : step_z + box_shape[2]]
                )
            summed = summed + (plane_weight * weight_y[step_y])[None] * along_z
        return summed

    summed = jnp.zeros((field_count,) + box_shape, jnp.float32)
    return lax.fori_loop(0, 9, one_plane, summed)


def divergence_of(velocity_pad):
    part_x = velocity_pad[0, 2:, 1:-1, 1:-1] - velocity_pad[0, :-2, 1:-1, 1:-1]
    part_y = velocity_pad[1, 1:-1, 2:, 1:-1] - velocity_pad[1, 1:-1, :-2, 1:-1]
    part_z = velocity_pad[2, 1:-1, 1:-1, 2:] - velocity_pad[2, 1:-1, 1:-1, :-2]
    return 0.5 * (part_x + part_y + part_z)


def gradient_of(pressure_pad):
    part_x = pressure_pad[2:, 1:-1, 1:-1] - pressure_pad[:-2, 1:-1, 1:-1]
    part_y = pressure_pad[1:-1, 2:, 1:-1] - pressure_pad[1:-1, :-2, 1:-1]
    part_z = pressure_pad[1:-1, 1:-1, 2:] - pressure_pad[1:-1, 1:-1, :-2]
    return 0.5 * jnp.stack([part_x, part_y, part_z], axis=0)


def restrict(field):
    return field.reshape(
        field.shape[0] // 2, 2, field.shape[1] // 2, 2, field.shape[2] // 2, 2
    ).mean(axis=(1, 3, 5))


def prolong(field):
    return jnp.repeat(jnp.repeat(jnp.repeat(field, 2, axis=0), 2, axis=1), 2, axis=2)


def inside_box(extents, margin):
    box_shape = (extents[0] + 2 * margin, extents[1] + 2 * margin, extents[2] + 2 * margin)
    coord_x = (
        lax.broadcasted_iota(jnp.int32, box_shape, 0) - margin + lax.axis_index("gx") * extents[0]
    )
    coord_y = (
        lax.broadcasted_iota(jnp.int32, box_shape, 1) - margin + lax.axis_index("gy") * extents[1]
    )
    coord_z = (
        lax.broadcasted_iota(jnp.int32, box_shape, 2) - margin + lax.axis_index("gz") * extents[2]
    )
    inside = (coord_x >= 0) & (coord_x < extents[0] * lax.axis_size("gx"))
    inside = inside & (coord_y >= 0) & (coord_y < extents[1] * lax.axis_size("gy"))
    inside = inside & (coord_z >= 0) & (coord_z < extents[2] * lax.axis_size("gz"))
    return inside


def smooth_level(source, spacing):
    relaxation = RELAX_WEIGHT / 6.0
    source_pad = padded_2(source, (("gx", 0), ("gy", 1), ("gz", 2)), 2)
    first_sweep = relaxation * spacing * source_pad
    second_wide = first_sweep[1:-1, 1:-1, 1:-1] + relaxation * (
        spacing * source_pad[1:-1, 1:-1, 1:-1] - operate(first_sweep)
    )
    second_wide = jnp.where(inside_box(source.shape, 1), second_wide, 0.0)
    residual = source - operate(second_wide) / spacing
    second_sweep = second_wide[1:-1, 1:-1, 1:-1]
    return (second_sweep, residual)


def solve_coarse(source):
    relaxation = RELAX_WEIGHT / 6.0
    spacing = 16.0
    first_sweep = relaxation * spacing * source
    first_pad = padded_2(first_sweep, (("gx", 0), ("gy", 1), ("gz", 2)), 1)
    return first_sweep + relaxation * (spacing * source - operate(first_pad))


def body(velocity, density, offsets, eighths):
    fields = jnp.concatenate([velocity, density[None]], axis=0)
    padded = padded_2(fields, (("gx", 1), ("gy", 2), ("gz", 3)), 4)
    advected = advect_block(padded, offsets, eighths)
    new_density = advected[3]
    moved_velocity = advected[:3]
    velocity_pad = padded_2(moved_velocity, (("gx", 1), ("gy", 2), ("gz", 3)), 1)
    divergence = divergence_of(velocity_pad)
    fine_sweep, fine_residual = smooth_level(-divergence, 1.0)
    middle_sweep, middle_residual = smooth_level(restrict(fine_residual), 4.0)
    coarse_sweep = solve_coarse(restrict(middle_residual))
    pressure = fine_sweep + prolong(middle_sweep + prolong(coarse_sweep))
    pressure_pad = padded_2(pressure, (("gx", 0), ("gy", 1), ("gz", 2)), 1)
    gradient = gradient_of(pressure_pad)
    return (moved_velocity - gradient, new_density, pressure)


def solution(mesh):
    return jax.shard_map(
        body,
        mesh=mesh,
        in_specs=(
            P(None, "gx", "gy", "gz"),
            P("gx", "gy", "gz"),
            P(None, "gx", "gy", "gz"),
            P(None, "gx", "gy", "gz"),
        ),
        out_specs=(P(None, "gx", "gy", "gz"), P("gx", "gy", "gz"), P("gx", "gy", "gz")),
        check_vma=False,
    )
```

profile of v0, /device:TPU:21, one launch (start us, length us, event | category | flops | bytes accessed | tf_op | source)
XLA Modules:
  0.0 275.3 jit_solution(4538477092353563090)
XLA Ops:
  1.6 3.2 %collective-permute-start = (f32[4,4,16,128]{3,2,1,0:T(8,128)S(1)}, f32[4,4,16,128]{3,2,1,0:T(8,128)S(1)}, u32[]{:S(2)}, u32[]{:S(2)}) collective-permute-start(f32[4,4,16,128]{3,2,1,0:T(8,128)S(1)} %get-tuple-element.195), channel_id=1, source_target_pairs={{0,8},{8,16},{16,24},{1,9},{9,17},{17,25},{2,10},{10,18},{18,26},{... | collective-permute-start | bytes 393224 | tf_op jit(solution)/shard_map/ppermute | solution.py:14
  4.8 2.1 collective-permute-start.1
  7.9 2.6 collective-permute-done.1
  11.6 3.1 %collective-permute-start.2 = (f32[4,16,4,128]{3,1,2,0:T(8,128)S(1)}, f32[4,16,4,128]{3,1,2,0:T(8,128)S(1)}, u32[]{:S(2)}, u32[]{:S(2)}) collective-permute-start(f32[4,16,4,128]{3,1,2,0:T(8,128)S(1)} %copy.159), channel_id=1, source_target_pairs={{0,2},{2,4},{4,6},{1,3},{3,5},{5,7},{8,10},{10,12},{12,14},{9,11},... | collective-permute-start | bytes 393224 | tf_op jit(solution)/shard_map/ppermute | solution.py:14
  14.8 3.1 %collective-permute-start.3 = (f32[4,16,4,128]{3,1,2,0:T(8,128)S(1)}, f32[4,16,4,128]{3,1,2,0:T(8,128)S(1)}, u32[]{:S(2)}, u32[]{:S(2)}) collective-permute-start(f32[4,16,4,128]{3,1,2,0:T(8,128)S(1)} %copy.160), channel_id=1, source_target_pairs={{2,0},{4,2},{6,4},{3,1},{5,3},{7,5},{10,8},{12,10},{14,12},{11,9},... | collective-permute-start | bytes 393224 | tf_op jit(solution)/shard_map/ppermute | solution.py:17
  18.8 2.9 %copy.144 = f32[4,16,16,128]{2,1,3,0:T(8,128)} copy(f32[4,16,16,128]{3,2,1,0:T(8,128)S(1)} %pad_maximum_fusion.2) | data formatting | bytes 1048576 | tf_op jit(solution)/shard_map/concatenate | solution.py:18
  21.7 3.0 %copy.143 = f32[4,16,4,128]{2,1,3,0:T(8,128)} copy(f32[4,16,4,128]{3,1,2,0:T(8,128)S(1)} %collective-permute-done.2) | data formatting | bytes 262144 | tf_op jit(solution)/shard_map/ppermute | solution.py:14
  24.7 2.9 %copy.145 = f32[4,16,4,128]{2,1,3,0:T(8,128)} copy(f32[4,16,4,128]{3,1,2,0:T(8,128)S(1)} %collective-permute-done.3) | data formatting | bytes 262144 | tf_op jit(solution)/shard_map/ppermute | solution.py:17
  27.6 6.9 %pad_maximum_fusion = f32[4,16,24,128]{2,1,3,0:T(8,128)S(1)} fusion(f32[4,16,4,128]{2,1,3,0:T(8,128)} %copy.145, f32[4,16,16,128]{2,1,3,0:T(8,128)} %copy.144, f32[4,16,4,128]{2,1,3,0:T(8,128)} %copy.143), kind=kLoop, calls=%fused_computation.189 | loop fusion | flops 393216 | bytes 1572864 | tf_op jit(solution)/shard_map/concatenate | solution.py:18
  35.8 4.6 %collective-permute-start.5 = (f32[4,16,24,4]{2,1,3,0:T(8,128)S(1)}, f32[4,16,24,4]{2,1,3,0:T(8,128)S(1)}, u32[]{:S(2)}, u32[]{:S(2)}) collective-permute-start(f32[4,16,24,4]{2,1,3,0:T(8,128)S(1)} %get-tuple-element.188), channel_id=1, source_target_pairs={{1,0},{3,2},{5,4},{7,6},{9,8},{11,10},{13,12},{15,14},{17,16},{19,... | collective-permute-start | bytes 73736 | tf_op jit(solution)/shard_map/ppermute | solution.py:17
  41.6 3.8 %copy.147 = f32[4,16,24,128]{3,2,1,0:T(8,128)} copy(f32[4,16,24,128]{2,1,3,0:T(8,128)} %copy-done) | data formatting | bytes 1572864 | tf_op jit(solution)/shard_map/concatenate | solution.py:18
  48.1 2.3 pad_maximum_fusion.1
  50.4 99.9 %while.14 = (s32[]{:T(128)}, f32[4,8,16,128]{3,2,1,0:T(8,128)S(1)}, f32[9,8,16,128]{3,2,1,0:T(8,128)}, f32[9,8,16,128]{3,2,1,0:T(8,128)S(1)}, f32[9,8,16,128]{3,...) while((s32[]{:T(128)}, f32[4,8,16,128]{3,2,1,0:T(8,128)S(1)}, ...), condition=%wide.region_1.2_spmd.clone, body=%wide.region_0.1_spmd.clone.sunk | while | flops 11419659 | bytes 25362724 | solution.py:63
  52.7 8.7 %fusion.152 = f32[4,8,16,128]{3,2,1,0:T(8,128)S(1)} fusion(f32[4,16,24,136]{3,2,1,0:T(8,128)S(1)} %get-tuple-element.359, s32[]{:T(128)} %get-tuple-element.338, s32[]{:T(128)S(6)} %add.1645, s32[]{:T(128)S(6)} %add.1646, s32[]{:T(128)S(6)} %add.1647, s32[]{:T(128)S(6)} %add.1648, s32[]{:T(128)S(6)} %add.1649, s32[]{:T(128)S(6)} %add.1650, ...), kind=kLoop, calls=%fused_computation.3.clone.1 | loop fusion | flops 11272192 | bytes 22937636 | tf_op jit(solution)/shard_map/while/body/eval_jaxpr/add | solution.py:59
  63.8 8.8 %fusion.152 = f32[4,8,16,128]{3,2,1,0:T(8,128)S(1)} fusion(f32[4,16,24,136]{3,2,1,0:T(8,128)S(1)} %get-tuple-element.359, s32[]{:T(128)} %get-tuple-element.338, s32[]{:T(128)S(6)} %add.1645, s32[]{:T(128)S(6)} %add.1646, s32[]{:T(128)S(6)} %add.1647, s32[]{:T(128)S(6)} %add.1648, s32[]{:T(128)S(6)} %add.1649, s32[]{:T(128)S(6)} %add.1650, ...), kind=kLoop, calls=%fused_computation.3.clone.1 | loop fusion | flops 11272192 | bytes 22937636 | tf_op jit(solution)/shard_map/while/body/eval_jaxpr/add | solution.py:59
  75.0 8.7 %fusion.152 = f32[4,8,16,128]{3,2,1,0:T(8,128)S(1)} fusion(f32[4,16,24,136]{3,2,1,0:T(8,128)S(1)} %get-tuple-element.359, s32[]{:T(128)} %get-tuple-element.338, s32[]{:T(128)S(6)} %add.1645, s32[]{:T(128)S(6)} %add.1646, s32[]{:T(128)S(6)} %add.1647, s32[]{:T(128)S(6)} %add.1648, s32[]{:T(128)S(6)} %add.1649, s32[]{:T(128)S(6)} %add.1650, ...), kind=kLoop, calls=%fused_computation.3.clone.1 | loop fusion | flops 11272192 | bytes 22937636 | tf_op jit(solution)/shard_map/while/body/eval_jaxpr/add | solution.py:59
  86.0 8.8 %fusion.152 = f32[4,8,16,128]{3,2,1,0:T(8,128)S(1)} fusion(f32[4,16,24,136]{3,2,1,0:T(8,128)S(1)} %get-tuple-element.359, s32[]{:T(128)} %get-tuple-element.338, s32[]{:T(128)S(6)} %add.1645, s32[]{:T(128)S(6)} %add.1646, s32[]{:T(128)S(6)} %add.1647, s32[]{:T(128)S(6)} %add.1648, s32[]{:T(128)S(6)} %add.1649, s32[]{:T(128)S(6)} %add.1650, ...), kind=kLoop, calls=%fused_computation.3.clone.1 | loop fusion | flops 11272192 | bytes 22937636 | tf_op jit(solution)/shard_map/while/body/eval_jaxpr/add | solution.py:59
  97.2 8.7 %fusion.152 = f32[4,8,16,128]{3,2,1,0:T(8,128)S(1)} fusion(f32[4,16,24,136]{3,2,1,0:T(8,128)S(1)} %get-tuple-element.359, s32[]{:T(128)} %get-tuple-element.338, s32[]{:T(128)S(6)} %add.1645, s32[]{:T(128)S(6)} %add.1646, s32[]{:T(128)S(6)} %add.1647, s32[]{:T(128)S(6)} %add.1648, s32[]{:T(128)S(6)} %add.1649, s32[]{:T(128)S(6)} %add.1650, ...), kind=kLoop, calls=%fused_computation.3.clone.1 | loop fusion | flops 11272192 | bytes 22937636 | tf_op jit(solution)/shard_map/while/body/eval_jaxpr/add | solution.py:59
  108.2 8.8 %fusion.152 = f32[4,8,16,128]{3,2,1,0:T(8,128)S(1)} fusion(f32[4,16,24,136]{3,2,1,0:T(8,128)S(1)} %get-tuple-element.359, s32[]{:T(128)} %get-tuple-element.338, s32[]{:T(128)S(6)} %add.1645, s32[]{:T(128)S(6)} %add.1646, s32[]{:T(128)S(6)} %add.1647, s32[]{:T(128)S(6)} %add.1648, s32[]{:T(128)S(6)} %add.1649, s32[]{:T(128)S(6)} %add.1650, ...), kind=kLoop, calls=%fused_computation.3.clone.1 | loop fusion | flops 11272192 | bytes 22937636 | tf_op jit(solution)/shard_map/while/body/eval_jaxpr/add | solution.py:59
  119.4 8.7 %fusion.152 = f32[4,8,16,128]{3,2,1,0:T(8,128)S(1)} fusion(f32[4,16,24,136]{3,2,1,0:T(8,128)S(1)} %get-tuple-element.359, s32[]{:T(128)} %get-tuple-element.338, s32[]{:T(128)S(6)} %add.1645, s32[]{:T(128)S(6)} %add.1646, s32[]{:T(128)S(6)} %add.1647, s32[]{:T(128)S(6)} %add.1648, s32[]{:T(128)S(6)} %add.1649, s32[]{:T(128)S(6)} %add.1650, ...), kind=kLoop, calls=%fused_computation.3.clone.1 | loop fusion | flops 11272192 | bytes 22937636 | tf_op jit(solution)/shard_map/while/body/eval_jaxpr/add | solution.py:59
  130.5 8.8 %fusion.152 = f32[4,8,16,128]{3,2,1,0:T(8,128)S(1)} fusion(f32[4,16,24,136]{3,2,1,0:T(8,128)S(1)} %get-tuple-element.359, s32[]{:T(128)} %get-tuple-element.338, s32[]{:T(128)S(6)} %add.1645, s32[]{:T(128)S(6)} %add.1646, s32[]{:T(128)S(6)} %add.1647, s32[]{:T(128)S(6)} %add.1648, s32[]{:T(128)S(6)} %add.1649, s32[]{:T(128)S(6)} %add.1650, ...), kind=kLoop, calls=%fused_computation.3.clone.1 | loop fusion | flops 11272192 | bytes 22937636 | tf_op jit(solution)/shard_map/while/body/eval_jaxpr/add | solution.py:59
  141.6 8.7 %fusion.152 = f32[4,8,16,128]{3,2,1,0:T(8,128)S(1)} fusion(f32[4,16,24,136]{3,2,1,0:T(8,128)S(1)} %get-tuple-element.359, s32[]{:T(128)} %get-tuple-element.338, s32[]{:T(128)S(6)} %add.1645, s32[]{:T(128)S(6)} %add.1646, s32[]{:T(128)S(6)} %add.1647, s32[]{:T(128)S(6)} %add.1648, s32[]{:T(128)S(6)} %add.1649, s32[]{:T(128)S(6)} %add.1650, ...), kind=kLoop, calls=%fused_computation.3.clone.1 | loop fusion | flops 11272192 | bytes 22937636 | tf_op jit(solution)/shard_map/while/body/eval_jaxpr/add | solution.py:59
  150.3 2.1 collective-permute-start.6
  152.4 3.2 %collective-permute-start.7 = (f32[3,1,16,128]{3,2,1,0:T(8,128)S(1)}, f32[3,1,16,128]{3,2,1,0:T(8,128)S(1)}, u32[]{:S(2)}, u32[]{:S(2)}) collective-permute-start(f32[3,1,16,128]{3,2,1,0:T(8,128)S(1)} %get-tuple-element.193), channel_id=1, source_target_pairs={{0,8},{8,16},{16,24},{1,9},{9,17},{17,25},{2,10},{10,18},{18,26},{... | collective-permute-start | bytes 73736 | tf_op jit(solution)/shard_map/ppermute | solution.py:14
  157.5 2.2 collective-permute-start.8
  159.6 3.3 %collective-permute-start.9 = (f32[3,10,1,128]{3,2,1,0:T(1,128)S(1)}, f32[3,10,1,128]{3,2,1,0:T(1,128)S(1)}, u32[]{:S(2)}, u32[]{:S(2)}) collective-permute-start(f32[3,10,1,128]{3,2,1,0:T(1,128)S(1)} %get-tuple-element.197), channel_id=1, source_target_pairs={{0,2},{2,4},{4,6},{1,3},{3,5},{5,7},{8,10},{10,12},{12,14},{9,11},... | collective-permute-start | bytes 46088 | tf_op jit(solution)/shard_map/ppermute | solution.py:14
  165.3 3.9 %collective-permute-start.10 = (f32[3,10,18,1]{3,2,1,0:T(8,128)S(1)}, f32[3,10,18,1]{3,2,1,0:T(8,128)S(1)}, u32[]{:S(2)}, u32[]{:S(2)}) collective-permute-start(f32[3,10,18,1]{3,2,1,0:T(8,128)S(1)} %get-tuple-element.191), channel_id=1, source_target_pairs={{1,0},{3,2},{5,4},{7,6},{9,8},{11,10},{13,12},{15,14},{17,16},{19,... | collective-permute-start | bytes 6488 | tf_op jit(solution)/shard_map/ppermute | solution.py:17
  170.4 2.3 collective-permute-done.11
  172.9 3.2 %collective-permute-start.12 = (f32[2,16,128]{2,1,0:T(8,128)S(1)}, f32[2,16,128]{2,1,0:T(8,128)S(1)}, u32[]{:S(2)}, u32[]{:S(2)}) collective-permute-start(f32[2,16,128]{2,1,0:T(8,128)S(1)} %get-tuple-element.220), channel_id=1, source_target_pairs={{0,8},{8,16},{16,24},{1,9},{9,17},{17,25},{2,10},{10,18},{18,26},{... | collective-permute-start | bytes 49160 | tf_op jit(solution)/shard_map/ppermute | solution.py:14
  176.1 2.1 collective-permute-start.13
  178.2 2.4 collective-permute-done.13
  180.6 2.2 collective-permute-start.14
  182.8 4.0 %collective-permute-start.15 = (f32[12,2,128]{2,1,0:T(2,128)S(1)}, f32[12,2,128]{2,1,0:T(2,128)S(1)}, u32[]{:S(2)}, u32[]{:S(2)}) collective-permute-start(f32[12,2,128]{2,1,0:T(2,128)S(1)} %get-tuple-element.213), channel_id=1, source_target_pairs={{2,0},{4,2},{6,4},{3,1},{5,3},{7,5},{10,8},{12,10},{14,12},{11,9},... | collective-permute-start | bytes 36872 | tf_op jit(solution)/shard_map/ppermute | solution.py:17
  189.0 4.6 %collective-permute-start.17 = (f32[12,20,2]{2,1,0:T(8,128)S(1)}, f32[12,20,2]{2,1,0:T(8,128)S(1)}, u32[]{:S(2)}, u32[]{:S(2)}) collective-permute-start(f32[12,20,2]{2,1,0:T(8,128)S(1)} %get-tuple-element.209), channel_id=1, source_target_pairs={{1,0},{3,2},{5,4},{7,6},{9,8},{11,10},{13,12},{15,14},{17,16},{19,... | collective-permute-start | bytes 5768 | tf_op jit(solution)/shard_map/ppermute | solution.py:17
  195.6 5.6 %reshape.46 = f32[4,2,8,2,64,2]{5,4,3,2,1,0:T(8,128)} reshape(f32[8,16,128]{2,1,0:T(8,128)S(1)} %fusion.104) | data formatting | bytes 131072 | tf_op jit(solution)/shard_map/reshape | solution.py:81
  201.2 2.5 reduce_sum.18
  205.7 3.4 %collective-permute-start.19 = (f32[2,8,64]{2,1,0:T(8,128)S(1)}, f32[2,8,64]{2,1,0:T(8,128)S(1)}, u32[]{:S(2)}, u32[]{:S(2)}) collective-permute-start(f32[2,8,64]{2,1,0:T(8,128)S(1)} %get-tuple-element.231), channel_id=1, source_target_pairs={{8,0},{16,8},{24,16},{9,1},{17,9},{25,17},{10,2},{18,10},{26,18},{... | collective-permute-start | bytes 12296 | tf_op jit(solution)/shard_map/ppermute | solution.py:17
  212.0 4.8 %collective-permute-start.21 = (f32[8,2,64]{2,1,0:T(2,128)S(1)}, f32[8,2,64]{2,1,0:T(2,128)S(1)}, u32[]{:S(2)}, u32[]{:S(2)}) collective-permute-start(f32[8,2,64]{2,1,0:T(2,128)S(1)} %get-tuple-element.226), channel_id=1, source_target_pairs={{2,0},{4,2},{6,4},{3,1},{5,3},{7,5},{10,8},{12,10},{14,12},{11,9},... | collective-permute-start | bytes 12296 | tf_op jit(solution)/shard_map/ppermute | solution.py:17
  219.0 4.3 %collective-permute-start.23 = (f32[8,12,2]{2,0,1:T(8,128)S(1)}, f32[8,12,2]{2,0,1:T(8,128)S(1)}, u32[]{:S(2)}, u32[]{:S(2)}) collective-permute-start(f32[8,12,2]{2,0,1:T(8,128)S(1)} %get-tuple-element.225), channel_id=1, source_target_pairs={{1,0},{3,2},{5,4},{7,6},{9,8},{11,10},{13,12},{15,14},{17,16},{19,... | collective-permute-start | bytes 2312 | tf_op jit(solution)/shard_map/ppermute | solution.py:17
  225.2 3.6 %collective-permute-start.24 = (f32[1,4,32]{2,1,0:T(4,128)S(1)}, f32[1,4,32]{2,1,0:T(4,128)S(1)}, u32[]{:S(2)}, u32[]{:S(2)}) collective-permute-start(f32[1,4,32]{2,1,0:T(4,128)S(1)} %get-tuple-element.235), channel_id=1, source_target_pairs={{8,0},{16,8},{24,16},{9,1},{17,9},{25,17},{10,2},{18,10},{26,18},{... | collective-permute-start | bytes 1544 | tf_op jit(solution)/shard_map/ppermute | solution.py:17
  230.8 2.4 collective-permute-done.25
  233.2 4.8 %collective-permute-start.26 = (f32[4,1,32]{2,1,0:T(1,128)S(1)}, f32[4,1,32]{2,1,0:T(1,128)S(1)}, u32[]{:S(2)}, u32[]{:S(2)}) collective-permute-start(f32[4,1,32]{2,1,0:T(1,128)S(1)} %get-tuple-element.233), channel_id=1, source_target_pairs={{2,0},{4,2},{6,4},{3,1},{5,3},{7,5},{10,8},{12,10},{14,12},{11,9},... | collective-permute-start | bytes 1544 | tf_op jit(solution)/shard_map/ppermute | solution.py:17
  240.0 3.3 %collective-permute-done.27 = f32[4,1,32]{2,1,0:T(1,128)S(1)} collective-permute-done((f32[4,1,32]{2,1,0:T(1,128)S(1)}, f32[4,1,32]{2,1,0:T(1,128)S(1)}, u32[]{:S(2)}, u32[]{:S(2)}) %collective-permute-start.27) | collective-permute-done | bytes 544 | tf_op jit(solution)/shard_map/ppermute | solution.py:14
  243.3 5.1 %collective-permute-start.28 = (f32[4,6,1]{2,1,0:T(8,128)S(1)}, f32[4,6,1]{2,1,0:T(8,128)S(1)}, u32[]{:S(2)}, u32[]{:S(2)}) collective-permute-start(f32[4,6,1]{2,1,0:T(8,128)S(1)} %get-tuple-element.228), channel_id=1, source_target_pairs={{1,0},{3,2},{5,4},{7,6},{9,8},{11,10},{13,12},{15,14},{17,16},{19,... | collective-permute-start | bytes 296 | tf_op jit(solution)/shard_map/ppermute | solution.py:17
  252.5 2.1 collective-permute-start.30
  254.6 3.2 %collective-permute-start.31 = (f32[1,16,128]{2,1,0:T(8,128)S(1)}, f32[1,16,128]{2,1,0:T(8,128)S(1)}, u32[]{:S(2)}, u32[]{:S(2)}) collective-permute-start(f32[1,16,128]{2,1,0:T(8,128)S(1)} %get-tuple-element.218), channel_id=1, source_target_pairs={{0,8},{8,16},{16,24},{1,9},{9,17},{17,25},{2,10},{10,18},{18,26},{... | collective-permute-start | bytes 24584 | tf_op jit(solution)/shard_map/ppermute | solution.py:14
  260.9 3.4 %collective-permute-start.33 = (f32[10,1,128]{2,1,0:T(1,128)S(1)}, f32[10,1,128]{2,1,0:T(1,128)S(1)}, u32[]{:S(2)}, u32[]{:S(2)}) collective-permute-start(f32[10,1,128]{2,1,0:T(1,128)S(1)} %get-tuple-element.216), channel_id=1, source_target_pairs={{0,2},{2,4},{4,6},{1,3},{3,5},{5,7},{8,10},{10,12},{12,14},{9,11},... | collective-permute-start | bytes 15368 | tf_op jit(solution)/shard_map/ppermute | solution.py:14
  266.3 4.9 %collective-permute-start.34 = (f32[10,18,1]{2,1,0:T(8,128)S(1)}, f32[10,18,1]{2,1,0:T(8,128)S(1)}, u32[]{:S(2)}, u32[]{:S(2)}) collective-permute-start(f32[10,18,1]{2,1,0:T(8,128)S(1)} %get-tuple-element.210), channel_id=1, source_target_pairs={{1,0},{3,2},{5,4},{7,6},{9,8},{11,10},{13,12},{15,14},{17,16},{19,... | collective-permute-start | bytes 2168 | tf_op jit(solution)/shard_map/ppermute | solution.py:17
  (138 shorter events, 65.7 us)
Async XLA Ops:
  1.6 6.3 %collective-permute-start = (f32[4,4,16,128]{3,2,1,0:T(8,128)S(1)}, f32[4,4,16,128]{3,2,1,0:T(8,128)S(1)}, u32[]{:S(2)}, u32[]{:S(2)}) collective-permute-start(f32[4,4,16,128]{3,2,1,0:T(8,128)S(1)} %get-tuple-element.195), channel_id=1, source_target_pairs={{0,8},{8,16},{16,24},{1,9},{9,17},{17,25},{2,10},{10,18},{18,26},{... | collective-permute-start | bytes 393224 | tf_op jit(solution)/shard_map/ppermute | solution.py:14
  4.8 5.7 %collective-permute-start.1 = (f32[4,4,16,128]{3,2,1,0:T(8,128)S(1)}, f32[4,4,16,128]{3,2,1,0:T(8,128)S(1)}, u32[]{:S(2)}, u32[]{:S(2)}) collective-permute-start(f32[4,4,16,128]{3,2,1,0:T(8,128)S(1)} %get-tuple-element.196), channel_id=1, source_target_pairs={{8,0},{16,8},{24,16},{9,1},{17,9},{25,17},{10,2},{18,10},{26,18},{... | collective-permute-start | bytes 393224 | tf_op jit(solution)/shard_map/ppermute | solution.py:17
  11.6 10.1 %collective-permute-start.2 = (f32[4,16,4,128]{3,1,2,0:T(8,128)S(1)}, f32[4,16,4,128]{3,1,2,0:T(8,128)S(1)}, u32[]{:S(2)}, u32[]{:S(2)}) collective-permute-start(f32[4,16,4,128]{3,1,2,0:T(8,128)S(1)} %copy.159), channel_id=1, source_target_pairs={{0,2},{2,4},{4,6},{1,3},{3,5},{5,7},{8,10},{10,12},{12,14},{9,11},... | collective-permute-start | bytes 393224 | tf_op jit(solution)/shard_map/ppermute | solution.py:14
  14.8 9.9 %collective-permute-start.3 = (f32[4,16,4,128]{3,1,2,0:T(8,128)S(1)}, f32[4,16,4,128]{3,1,2,0:T(8,128)S(1)}, u32[]{:S(2)}, u32[]{:S(2)}) collective-permute-start(f32[4,16,4,128]{3,1,2,0:T(8,128)S(1)} %copy.160), channel_id=1, source_target_pairs={{2,0},{4,2},{6,4},{3,1},{5,3},{7,5},{10,8},{12,10},{14,12},{11,9},... | collective-permute-start | bytes 393224 | tf_op jit(solution)/shard_map/ppermute | solution.py:17
  34.5 5.9 %copy-start = (f32[4,16,24,128]{2,1,3,0:T(8,128)}, f32[4,16,24,128]{2,1,3,0:T(8,128)S(1)}, u32[]{:S(2)}) copy-start(f32[4,16,24,128]{2,1,3,0:T(8,128)S(1)} %pad_maximum_fusion) | copy-start | bytes 2359300
  34.5 10.9 %collective-permute-start.4 = (f32[4,16,24,4]{2,1,3,0:T(8,128)S(1)}, f32[4,16,24,4]{2,1,3,0:T(8,128)S(1)}, u32[]{:S(2)}, u32[]{:S(2)}) collective-permute-start(f32[4,16,24,4]{2,1,3,0:T(8,128)S(1)} %get-tuple-element.187), channel_id=1, source_target_pairs={{0,1},{2,3},{4,5},{6,7},{8,9},{10,11},{12,13},{14,15},{16,17},{18,... | collective-permute-start | bytes 73736 | tf_op jit(solution)/shard_map/ppermute | solution.py:14
  35.8 10.9 %collective-permute-start.5 = (f32[4,16,24,4]{2,1,3,0:T(8,128)S(1)}, f32[4,16,24,4]{2,1,3,0:T(8,128)S(1)}, u32[]{:S(2)}, u32[]{:S(2)}) collective-permute-start(f32[4,16,24,4]{2,1,3,0:T(8,128)S(1)} %get-tuple-element.188), channel_id=1, source_target_pairs={{1,0},{3,2},{5,4},{7,6},{9,8},{11,10},{13,12},{15,14},{17,16},{19,... | collective-permute-start | bytes 73736 | tf_op jit(solution)/shard_map/ppermute | solution.py:17
  150.3 5.3 %collective-permute-start.6 = (f32[3,1,16,128]{3,2,1,0:T(8,128)S(1)}, f32[3,1,16,128]{3,2,1,0:T(8,128)S(1)}, u32[]{:S(2)}, u32[]{:S(2)}) collective-permute-start(f32[3,1,16,128]{3,2,1,0:T(8,128)S(1)} %get-tuple-element.194), channel_id=1, source_target_pairs={{8,0},{16,8},{24,16},{9,1},{17,9},{25,17},{10,2},{18,10},{26,18},{... | collective-permute-start | bytes 73736 | tf_op jit(solution)/shard_map/ppermute | solution.py:17
  152.4 5.0 %collective-permute-start.7 = (f32[3,1,16,128]{3,2,1,0:T(8,128)S(1)}, f32[3,1,16,128]{3,2,1,0:T(8,128)S(1)}, u32[]{:S(2)}, u32[]{:S(2)}) collective-permute-start(f32[3,1,16,128]{3,2,1,0:T(8,128)S(1)} %get-tuple-element.193), channel_id=1, source_target_pairs={{0,8},{8,16},{16,24},{1,9},{9,17},{17,25},{2,10},{10,18},{18,26},{... | collective-permute-start | bytes 73736 | tf_op jit(solution)/shard_map/ppermute | solution.py:14
  157.5 5.5 %collective-permute-start.8 = (f32[3,10,1,128]{3,2,1,0:T(1,128)S(1)}, f32[3,10,1,128]{3,2,1,0:T(1,128)S(1)}, u32[]{:S(2)}, u32[]{:S(2)}) collective-permute-start(f32[3,10,1,128]{3,2,1,0:T(1,128)S(1)} %get-tuple-element.198), channel_id=1, source_target_pairs={{2,0},{4,2},{6,4},{3,1},{5,3},{7,5},{10,8},{12,10},{14,12},{11,9},... | collective-permute-start | bytes 46088 | tf_op jit(solution)/shard_map/ppermute | solution.py:17
  159.6 5.4 %collective-permute-start.9 = (f32[3,10,1,128]{3,2,1,0:T(1,128)S(1)}, f32[3,10,1,128]{3,2,1,0:T(1,128)S(1)}, u32[]{:S(2)}, u32[]{:S(2)}) collective-permute-start(f32[3,10,1,128]{3,2,1,0:T(1,128)S(1)} %get-tuple-element.197), channel_id=1, source_target_pairs={{0,2},{2,4},{4,6},{1,3},{3,5},{5,7},{8,10},{10,12},{12,14},{9,11},... | collective-permute-start | bytes 46088 | tf_op jit(solution)/shard_map/ppermute | solution.py:14
  165.3 5.2 %collective-permute-start.10 = (f32[3,10,18,1]{3,2,1,0:T(8,128)S(1)}, f32[3,10,18,1]{3,2,1,0:T(8,128)S(1)}, u32[]{:S(2)}, u32[]{:S(2)}) collective-permute-start(f32[3,10,18,1]{3,2,1,0:T(8,128)S(1)} %get-tuple-element.191), channel_id=1, source_target_pairs={{1,0},{3,2},{5,4},{7,6},{9,8},{11,10},{13,12},{15,14},{17,16},{19,... | collective-permute-start | bytes 6488 | tf_op jit(solution)/shard_map/ppermute | solution.py:17
  169.1 3.6 %collective-permute-start.11 = (f32[3,10,18,1]{3,2,1,0:T(8,128)S(1)}, f32[3,10,18,1]{3,2,1,0:T(8,128)S(1)}, u32[]{:S(2)}, u32[]{:S(2)}) collective-permute-start(f32[3,10,18,1]{3,2,1,0:T(8,128)S(1)} %get-tuple-element.192), channel_id=1, source_target_pairs={{0,1},{2,3},{4,5},{6,7},{8,9},{10,11},{12,13},{14,15},{16,17},{18,... | collective-permute-start | bytes 6488 | tf_op jit(solution)/shard_map/ppermute | solution.py:14
  172.9 5.3 %collective-permute-start.12 = (f32[2,16,128]{2,1,0:T(8,128)S(1)}, f32[2,16,128]{2,1,0:T(8,128)S(1)}, u32[]{:S(2)}, u32[]{:S(2)}) collective-permute-start(f32[2,16,128]{2,1,0:T(8,128)S(1)} %get-tuple-element.220), channel_id=1, source_target_pairs={{0,8},{8,16},{16,24},{1,9},{9,17},{17,25},{2,10},{10,18},{18,26},{... | collective-permute-start | bytes 49160 | tf_op jit(solution)/shard_map/ppermute | solution.py:14
  176.1 4.5 %collective-permute-start.13 = (f32[2,16,128]{2,1,0:T(8,128)S(1)}, f32[2,16,128]{2,1,0:T(8,128)S(1)}, u32[]{:S(2)}, u32[]{:S(2)}) collective-permute-start(f32[2,16,128]{2,1,0:T(8,128)S(1)} %get-tuple-element.221), channel_id=1, source_target_pairs={{8,0},{16,8},{24,16},{9,1},{17,9},{25,17},{10,2},{18,10},{26,18},{... | collective-permute-start | bytes 49160 | tf_op jit(solution)/shard_map/ppermute | solution.py:17
  180.6 6.2 %collective-permute-start.14 = (f32[12,2,128]{2,1,0:T(2,128)S(1)}, f32[12,2,128]{2,1,0:T(2,128)S(1)}, u32[]{:S(2)}, u32[]{:S(2)}) collective-permute-start(f32[12,2,128]{2,1,0:T(2,128)S(1)} %get-tuple-element.212), channel_id=1, source_target_pairs={{0,2},{2,4},{4,6},{1,3},{3,5},{5,7},{8,10},{10,12},{12,14},{9,11},... | collective-permute-start | bytes 36872 | tf_op jit(solution)/shard_map/ppermute | solution.py:14
  182.8 4.8 %collective-permute-start.15 = (f32[12,2,128]{2,1,0:T(2,128)S(1)}, f32[12,2,128]{2,1,0:T(2,128)S(1)}, u32[]{:S(2)}, u32[]{:S(2)}) collective-permute-start(f32[12,2,128]{2,1,0:T(2,128)S(1)} %get-tuple-element.213), channel_id=1, source_target_pairs={{2,0},{4,2},{6,4},{3,1},{5,3},{7,5},{10,8},{12,10},{14,12},{11,9},... | collective-permute-start | bytes 36872 | tf_op jit(solution)/shard_map/ppermute | solution.py:17
  187.7 5.9 %collective-permute-start.16 = (f32[12,20,2]{2,1,0:T(8,128)S(1)}, f32[12,20,2]{2,1,0:T(8,128)S(1)}, u32[]{:S(2)}, u32[]{:S(2)}) collective-permute-start(f32[12,20,2]{2,1,0:T(8,128)S(1)} %get-tuple-element.208), channel_id=1, source_target_pairs={{0,1},{2,3},{4,5},{6,7},{8,9},{10,11},{12,13},{14,15},{16,17},{18,... | collective-permute-start | bytes 5768 | tf_op jit(solution)/shard_map/ppermute | solution.py:14
  189.0 5.6 %collective-permute-start.17 = (f32[12,20,2]{2,1,0:T(8,128)S(1)}, f32[12,20,2]{2,1,0:T(8,128)S(1)}, u32[]{:S(2)}, u32[]{:S(2)}) collective-permute-start(f32[12,20,2]{2,1,0:T(8,128)S(1)} %get-tuple-element.209), channel_id=1, source_target_pairs={{1,0},{3,2},{5,4},{7,6},{9,8},{11,10},{13,12},{15,14},{17,16},{19,... | collective-permute-start | bytes 5768 | tf_op jit(solution)/shard_map/ppermute | solution.py:17
  203.7 5.3 %collective-permute-start.18 = (f32[2,8,64]{2,1,0:T(8,128)S(1)}, f32[2,8,64]{2,1,0:T(8,128)S(1)}, u32[]{:S(2)}, u32[]{:S(2)}) collective-permute-start(f32[2,8,64]{2,1,0:T(8,128)S(1)} %get-tuple-element.230), channel_id=1, source_target_pairs={{0,8},{8,16},{16,24},{1,9},{9,17},{17,25},{2,10},{10,18},{18,26},{... | collective-permute-start | bytes 12296 | tf_op jit(solution)/shard_map/ppermute | solution.py:14
  205.7 4.4 %collective-permute-start.19 = (f32[2,8,64]{2,1,0:T(8,128)S(1)}, f32[2,8,64]{2,1,0:T(8,128)S(1)}, u32[]{:S(2)}, u32[]{:S(2)}) collective-permute-start(f32[2,8,64]{2,1,0:T(8,128)S(1)} %get-tuple-element.231), channel_id=1, source_target_pairs={{8,0},{16,8},{24,16},{9,1},{17,9},{25,17},{10,2},{18,10},{26,18},{... | collective-permute-start | bytes 12296 | tf_op jit(solution)/shard_map/ppermute | solution.py:17
  210.1 6.8 %collective-permute-start.20 = (f32[8,2,64]{2,1,0:T(2,128)S(1)}, f32[8,2,64]{2,1,0:T(2,128)S(1)}, u32[]{:S(2)}, u32[]{:S(2)}) collective-permute-start(f32[8,2,64]{2,1,0:T(2,128)S(1)} %get-tuple-element.227), channel_id=1, source_target_pairs={{0,2},{2,4},{4,6},{1,3},{3,5},{5,7},{8,10},{10,12},{12,14},{9,11},... | collective-permute-start | bytes 12296 | tf_op jit(solution)/shard_map/ppermute | solution.py:14
  212.0 5.6 %collective-permute-start.21 = (f32[8,2,64]{2,1,0:T(2,128)S(1)}, f32[8,2,64]{2,1,0:T(2,128)S(1)}, u32[]{:S(2)}, u32[]{:S(2)}) collective-permute-start(f32[8,2,64]{2,1,0:T(2,128)S(1)} %get-tuple-element.226), channel_id=1, source_target_pairs={{2,0},{4,2},{6,4},{3,1},{5,3},{7,5},{10,8},{12,10},{14,12},{11,9},... | collective-permute-start | bytes 12296 | tf_op jit(solution)/shard_map/ppermute | solution.py:17
  217.7 5.6 %collective-permute-start.22 = (f32[8,12,2]{2,0,1:T(8,128)S(1)}, f32[8,12,2]{2,0,1:T(8,128)S(1)}, u32[]{:S(2)}, u32[]{:S(2)}) collective-permute-start(f32[8,12,2]{2,0,1:T(8,128)S(1)} %get-tuple-element.224), channel_id=1, source_target_pairs={{0,1},{2,3},{4,5},{6,7},{8,9},{10,11},{12,13},{14,15},{16,17},{18,... | collective-permute-start | bytes 2312 | tf_op jit(solution)/shard_map/ppermute | solution.py:14
  219.0 5.1 %collective-permute-start.23 = (f32[8,12,2]{2,0,1:T(8,128)S(1)}, f32[8,12,2]{2,0,1:T(8,128)S(1)}, u32[]{:S(2)}, u32[]{:S(2)}) collective-permute-start(f32[8,12,2]{2,0,1:T(8,128)S(1)} %get-tuple-element.225), channel_id=1, source_target_pairs={{1,0},{3,2},{5,4},{7,6},{9,8},{11,10},{13,12},{15,14},{17,16},{19,... | collective-permute-start | bytes 2312 | tf_op jit(solution)/shard_map/ppermute | solution.py:17
  225.2 5.6 %collective-permute-start.24 = (f32[1,4,32]{2,1,0:T(4,128)S(1)}, f32[1,4,32]{2,1,0:T(4,128)S(1)}, u32[]{:S(2)}, u32[]{:S(2)}) collective-permute-start(f32[1,4,32]{2,1,0:T(4,128)S(1)} %get-tuple-element.235), channel_id=1, source_target_pairs={{8,0},{16,8},{24,16},{9,1},{17,9},{25,17},{10,2},{18,10},{26,18},{... | collective-permute-start | bytes 1544 | tf_op jit(solution)/shard_map/ppermute | solution.py:17
  228.9 4.3 %collective-permute-start.25 = (f32[1,4,32]{2,1,0:T(4,128)S(1)}, f32[1,4,32]{2,1,0:T(4,128)S(1)}, u32[]{:S(2)}, u32[]{:S(2)}) collective-permute-start(f32[1,4,32]{2,1,0:T(4,128)S(1)} %get-tuple-element.234), channel_id=1, source_target_pairs={{0,8},{8,16},{16,24},{1,9},{9,17},{17,25},{2,10},{10,18},{18,26},{... | collective-permute-start | bytes 1544 | tf_op jit(solution)/shard_map/ppermute | solution.py:14
  233.2 6.8 %collective-permute-start.26 = (f32[4,1,32]{2,1,0:T(1,128)S(1)}, f32[4,1,32]{2,1,0:T(1,128)S(1)}, u32[]{:S(2)}, u32[]{:S(2)}) collective-permute-start(f32[4,1,32]{2,1,0:T(1,128)S(1)} %get-tuple-element.233), channel_id=1, source_target_pairs={{2,0},{4,2},{6,4},{3,1},{5,3},{7,5},{10,8},{12,10},{14,12},{11,9},... | collective-permute-start | bytes 1544 | tf_op jit(solution)/shard_map/ppermute | solution.py:17
  238.0 5.2 %collective-permute-start.27 = (f32[4,1,32]{2,1,0:T(1,128)S(1)}, f32[4,1,32]{2,1,0:T(1,128)S(1)}, u32[]{:S(2)}, u32[]{:S(2)}) collective-permute-start(f32[4,1,32]{2,1,0:T(1,128)S(1)} %get-tuple-element.232), channel_id=1, source_target_pairs={{0,2},{2,4},{4,6},{1,3},{3,5},{5,7},{8,10},{10,12},{12,14},{9,11},... | collective-permute-start | bytes 1544 | tf_op jit(solution)/shard_map/ppermute | solution.py:14
  243.3 6.4 %collective-permute-start.28 = (f32[4,6,1]{2,1,0:T(8,128)S(1)}, f32[4,6,1]{2,1,0:T(8,128)S(1)}, u32[]{:S(2)}, u32[]{:S(2)}) collective-permute-start(f32[4,6,1]{2,1,0:T(8,128)S(1)} %get-tuple-element.228), channel_id=1, source_target_pairs={{1,0},{3,2},{5,4},{7,6},{9,8},{11,10},{13,12},{15,14},{17,16},{19,... | collective-permute-start | bytes 296 | tf_op jit(solution)/shard_map/ppermute | solution.py:17
  248.5 3.1 %collective-permute-start.29 = (f32[4,6,1]{2,1,0:T(8,128)S(1)}, f32[4,6,1]{2,1,0:T(8,128)S(1)}, u32[]{:S(2)}, u32[]{:S(2)}) collective-permute-start(f32[4,6,1]{2,1,0:T(8,128)S(1)} %get-tuple-element.229), channel_id=1, source_target_pairs={{0,1},{2,3},{4,5},{6,7},{8,9},{10,11},{12,13},{14,15},{16,17},{18,... | collective-permute-start | bytes 296 | tf_op jit(solution)/shard_map/ppermute | solution.py:14
  252.5 22.8 %copy-start.1 = (f32[8,16,128]{2,1,0:T(8,128)}, f32[8,16,128]{2,1,0:T(8,128)S(1)}, u32[]{:S(2)}) copy-start(f32[8,16,128]{2,1,0:T(8,128)S(1)} %slice_add_fusion.10) | copy-start | bytes 196612
  252.5 5.3 %collective-permute-start.30 = (f32[1,16,128]{2,1,0:T(8,128)S(1)}, f32[1,16,128]{2,1,0:T(8,128)S(1)}, u32[]{:S(2)}, u32[]{:S(2)}) collective-permute-start(f32[1,16,128]{2,1,0:T(8,128)S(1)} %get-tuple-element.219), channel_id=1, source_target_pairs={{8,0},{16,8},{24,16},{9,1},{17,9},{25,17},{10,2},{18,10},{26,18},{... | collective-permute-start | bytes 24584 | tf_op jit(solution)/shard_map/ppermute | solution.py:17
  254.6 4.4 %collective-permute-start.31 = (f32[1,16,128]{2,1,0:T(8,128)S(1)}, f32[1,16,128]{2,1,0:T(8,128)S(1)}, u32[]{:S(2)}, u32[]{:S(2)}) collective-permute-start(f32[1,16,128]{2,1,0:T(8,128)S(1)} %get-tuple-element.218), channel_id=1, source_target_pairs={{0,8},{8,16},{16,24},{1,9},{9,17},{17,25},{2,10},{10,18},{18,26},{... | collective-permute-start | bytes 24584 | tf_op jit(solution)/shard_map/ppermute | solution.py:14
  259.0 5.9 %collective-permute-start.32 = (f32[10,1,128]{2,1,0:T(1,128)S(1)}, f32[10,1,128]{2,1,0:T(1,128)S(1)}, u32[]{:S(2)}, u32[]{:S(2)}) collective-permute-start(f32[10,1,128]{2,1,0:T(1,128)S(1)} %get-tuple-element.217), channel_id=1, source_target_pairs={{2,0},{4,2},{6,4},{3,1},{5,3},{7,5},{10,8},{12,10},{14,12},{11,9},... | collective-permute-start | bytes 15368 | tf_op jit(solution)/shard_map/ppermute | solution.py:17
  260.9 5.3 %collective-permute-start.33 = (f32[10,1,128]{2,1,0:T(1,128)S(1)}, f32[10,1,128]{2,1,0:T(1,128)S(1)}, u32[]{:S(2)}, u32[]{:S(2)}) collective-permute-start(f32[10,1,128]{2,1,0:T(1,128)S(1)} %get-tuple-element.216), channel_id=1, source_target_pairs={{0,2},{2,4},{4,6},{1,3},{3,5},{5,7},{8,10},{10,12},{12,14},{9,11},... | collective-permute-start | bytes 15368 | tf_op jit(solution)/shard_map/ppermute | solution.py:14
  266.3 6.2 %collective-permute-start.34 = (f32[10,18,1]{2,1,0:T(8,128)S(1)}, f32[10,18,1]{2,1,0:T(8,128)S(1)}, u32[]{:S(2)}, u32[]{:S(2)}) collective-permute-start(f32[10,18,1]{2,1,0:T(8,128)S(1)} %get-tuple-element.210), channel_id=1, source_target_pairs={{1,0},{3,2},{5,4},{7,6},{9,8},{11,10},{13,12},{15,14},{17,16},{19,... | collective-permute-start | bytes 2168 | tf_op jit(solution)/shard_map/ppermute | solution.py:17
  271.2 3.2 %collective-permute-start.35 = (f32[10,18,1]{2,1,0:T(8,128)S(1)}, f32[10,18,1]{2,1,0:T(8,128)S(1)}, u32[]{:S(2)}, u32[]{:S(2)}) collective-permute-start(f32[10,18,1]{2,1,0:T(8,128)S(1)} %get-tuple-element.211), channel_id=1, source_target_pairs={{0,1},{2,3},{4,5},{6,7},{8,9},{10,11},{12,13},{14,15},{16,17},{18,... | collective-permute-start | bytes 2168 | tf_op jit(solution)/shard_map/ppermute | solution.py:14
where the time goes:
time: 278 us; the launch traced here: 275 us
  other arithmetic  111 us (40%)
  starting transfers between devices  104 us (37%)
  local copies, waits for them, and re-layouts  31.5 us (11%)
  waiting for transfers between devices  27.2 us (10%)
    add x9, other arithmetic, one_plane(): summed = summed + (plane_weight * weight_y[step_y])[None] * along_z  78.8 us
    ppermute x18, starting transfers between devices, padded_2(): lax.ppermute(lax.slice_in_dim(block, 0, width, axis=dim), axis, backward)  63.4 us
    ppermute x18, starting transfers between devices, padded_2(): lax.ppermute(lax.slice_in_dim(block, block.shape[dim] - width, None, axis...  40.2 us
    ppermute x18, waiting for transfers between devices, padded_2(): lax.ppermute(lax.slice_in_dim(block, block.shape[dim] - width, None, axis...  17.9 us
    mul x9, other arithmetic, one_plane(): summed = summed + (plane_weight * weight_y[step_y])[None] * along_z  13.7 us
    concatenate x13, other arithmetic, padded_2(): block = jnp.concatenate([low, block, high], axis=dim)  10.4 us
    ppermute x18, waiting for transfers between devices, padded_2(): lax.ppermute(lax.slice_in_dim(block, 0, width, axis=dim), axis, backward)  9.31 us
    mul x9, local copies, waits for them, and re-layouts, one_plane(): weight_z[step_z][None] * window[:, :, :, step_z:step_z + box_shape[2]]  7.2 us
  transfers between devices with their start and end apart: 36, of which 16 were waited for; matrix products, arithmetic and copies ran while one was open for 5% of the time, Pallas kernels for 0%

commit v1 on v0

v1 whole, which is shorter than its diff:
```python
import functools

import jax
import jax.numpy as jnp
from jax import lax
from jax.experimental import pallas as pl
from jax.experimental.pallas import tpu as pltpu
from jax.sharding import PartitionSpec as P

MESH = pl.DeviceIdType.MESH
RELAX = (6.0 / 7.0) / 6.0
HALO = 4
XY = [(dx, dy) for dx in (-1, 0, 1) for dy in (-1, 0, 1) if (dx, dy) != (0, 0)]
FAR = [(dx, dy) for dx in (-2, -1, 0, 1, 2) for dy in (-1, 0, 1) if (dx, dy) != (0, 0)]


def lanes(shape):
    return lax.broadcasted_iota(jnp.int32, shape, len(shape) - 1)


def roll(x, shift, axis):
    shift = shift % x.shape[axis]
    return x if shift == 0 else pltpu.roll(x, shift, axis)


def inside(sizes, me, delta):
    ok = None
    for n, i, d in zip(sizes, me, delta):
        if d:
            one = (i + d >= 0) & (i + d < n)
            ok = one if ok is None else ok & one
    return ok


class Comm:
    def __init__(self, sizes, me, send, recv):
        self.sizes, self.me, self.send, self.recv = sizes, me, send, recv
        self.copies = []

    def add(self, delta, src, dst, slot):
        device = tuple(i + d for i, d in zip(self.me, delta))
        copy = pltpu.make_async_remote_copy(
            src_ref=src, dst_ref=dst, send_sem=self.send.at[slot], recv_sem=self.recv.at[slot],
            device_id=device, device_id_type=MESH,
        )
        to = inside(self.sizes, self.me, delta)
        source = inside(self.sizes, self.me, tuple(-d for d in delta))
        pl.when(to)(copy.start)
        self.copies.append((copy, to, source))

    def wait(self):
        for copy, to, source in self.copies:
            pl.when(source)(copy.wait_recv)
        for copy, to, source in self.copies:
            pl.when(to)(copy.wait_send)


def zero_if_missing(sizes, me, delta, ref):
    @pl.when(jnp.logical_not(inside(sizes, me, delta)))
    def _():
        ref[...] = jnp.zeros(ref.shape, ref.dtype)


def pick_x(d):
    return {-1: 0, 1: 1}[d]


def exchange_xy(sizes, me, own, strips, rx, ry, rc, sems, out, zero=True):
    f, p, r, _ = own.shape
    for i in range(p):
        strips[0, :, i] = own[:, i, 0:HALO, :]
        strips[1, :, i] = own[:, i, r - HALO : r, :]
    comm = Comm(sizes, me, *sems)
    for slot, (dx, dy) in enumerate(XY):
        xs = slice(0, HALO) if dx < 0 else slice(p - HALO, p)
        if dy == 0:
            src, dst = own.at[:, xs], rx.at[pick_x(-dx)]
        elif dx == 0:
            src, dst = strips.at[pick_x(dy)], ry.at[pick_x(-dy)]
        else:
            src, dst = strips.at[pick_x(dy), :, xs], rc.at[pick_x(-dx), pick_x(-dy)]
        comm.add((dx, dy, 0), src, dst, slot)
    for dx, dy in XY:
        ref = rx.at[pick_x(dx)] if dy == 0 else ry.at[pick_x(dy)] if dx == 0 else rc.at[pick_x(dx), pick_x(dy)]
        zero_if_missing(sizes, me, (dx, dy, 0), ref)
    out[:, HALO : HALO + p, HALO : HALO + r, :] = own[...]
    comm.wait()
    for sx, xs in ((0, slice(0, HALO)), (1, slice(HALO + p, HALO + p + HALO))):
        out[:, xs, HALO : HALO + r, :] = rx[sx]
        for sy, ys in ((0, slice(0, HALO)), (1, slice(HALO + r, HALO + r + HALO))):
            out[:, xs, ys, :] = rc[sx, sy]
    for sy, ys in ((0, slice(0, HALO)), (1, slice(HALO + r, HALO + r + HALO))):
        out[:, HALO : HALO + p, ys, :] = ry[sy]


def exchange_z(sizes, me, own, got, sems):
    comm = Comm(sizes, me, *sems)
    comm.add((0, 0, -1), own, got.at[1], 0)
    comm.add((0, 0, 1), own, got.at[0], 1)
    zero_if_missing(sizes, me, (0, 0, -1), got.at[0])
    zero_if_missing(sizes, me, (0, 0, 1), got.at[1])
    comm.wait()


def pack_z(ext, packed):
    f, p, rows, _ = ext.shape
    lane = lanes((rows, 128))
    for c in range(f):
        total = roll(ext[c, 0], 4, 1)
        for x in range(1, p):
            total = jnp.where(lane >= 8 * x, roll(ext[c, x], 4 + 8 * x, 1), total)
        packed[c] = total


def gather(x, index):
    return jnp.take_along_axis(x, index, axis=1, mode="promise_in_bounds")


def advect_tile(code, load, shift):
    ox, oy, oz = code & 7, (code >> 3) & 7, (code >> 6) & 7
    fx = ((code >> 9) & 7).astype(jnp.float32) * 0.125
    fy = ((code >> 12) & 7).astype(jnp.float32) * 0.125
    fz = ((code >> 15) & 7).astype(jnp.float32) * 0.125
    low = (lanes((8, 128)) + oz + shift) & 127
    high = (low + 1) & 127

    def weight(o, frac, step):
        return jnp.where(o == step, 1.0 - frac, jnp.where(o == step - 1, frac, 0.0))

    wy = [weight(oy, fy, dy) for dy in range(9)]
    totals = [None] * 4
    for dx in range(9):
        wx = weight(ox, fx, dx)
        wx0, wx1 = wx * (1.0 - fz), wx * fz
        for c in range(4):
            a0 = a1 = None
            for dy in range(9):
                rows = load(c, dx, dy)
                g0, g1 = wy[dy] * gather(rows, low), wy[dy] * gather(rows, high)
                a0 = g0 if a0 is None else a0 + g0
                a1 = g1 if a1 is None else a1 + g1
            value = wx0 * a0 + wx1 * a1
            totals[c] = value if totals[c] is None else totals[c] + value
    return totals


def kernel(sizes, vel, den, off, eig, new_vel, new_den, press, fields, stripA, rxA, ryA, rcA, ext, packed,
           gotP, srcA, srcB, code, codeB, resB, u, stripB, rxB, ryB, rcB, extU, packU, gotU, wide, s0, q0, r0,
           tmp0, own1, strip1, rx1, ry1, rc1, ext1, got1, wide1, q1, r1, tmp1, own2, got2, ext2, gotz2, sum1, fine,
           sxyA, rxyA, szA, rzA, sxyB, rxyB, szB, rzB, sxy1, rxy1, sz1, rz1, sxy2, rxy2, sz2, rz2):
    me = tuple(lax.axis_index(a) for a in ("gx", "gy", "gz"))
    p, r = den.shape[0], den.shape[1]
    fields[0:3] = vel[...]
    fields[3] = den[...]

    barrier = pltpu.get_barrier_semaphore()
    peers = [(dx, dy, 0) for dx, dy in FAR] + [(0, 0, -1), (0, 0, 1)]
    count = jnp.int32(0)
    for delta in peers:
        ok = inside(sizes, me, delta)

        @pl.when(ok)
        def _():
            pl.semaphore_signal(barrier, inc=1, device_id=tuple(i + d for i, d in zip(me, delta)), device_id_type=MESH)

        count = count + jnp.where(ok, 1, 0)
    pl.semaphore_wait(barrier, count)

    whole = (off[0] + 4) + 8 * (off[1] + 4) + 64 * (off[2] + 4)
    code[...] = whole + 512 * eig[0] + 4096 * eig[1] + 32768 * eig[2]
    lane16 = lanes((r, 128))
    total = roll(code[0], 12, 1)
    for g in range(1, p):
        total = jnp.where(lane16 >= 16 * g, roll(code[g], 16 * g + 12, 1), total)
    codeB[...] = total

    exchange_xy(sizes, me, fields, stripA, rxA, ryA, rcA, (sxyA, rxyA), ext)
    pack_z(ext, packed)
    exchange_z(sizes, me, packed, gotP, (szA, rzA))

    rows = r + 8
    lane = lanes((rows, 128))
    for c in range(4):
        below, above = gotP[0, c], gotP[1, c]
        halves = []
        for h in range(2):
            total = None
            for g in range(8):
                x = 8 * h + g
                main = ext[c, x]
                srcA[c, x] = jnp.where(lane < 4, roll(below, -8 * x, 1), roll(main, 4, 1))
                piece = jnp.where((lane & 15) < 12, roll(main, 16 * g + 12, 1), roll(above, 8 * g + 8 - 64 * h, 1))
                total = piece if total is None else jnp.where(lane >= 16 * g, piece, total)
            halves.append(total)
        for dx in range(9):
            if dx == 8:
                srcB[c, dx] = halves[1]
            else:
                srcB[c, dx] = jnp.where(lane < 128 - 16 * dx, roll(halves[0], -16 * dx, 1), roll(halves[1], -16 * dx, 1))

    for half in range(r // 8):
        y0 = 8 * half
        totals = advect_tile(codeB[y0 : y0 + 8], lambda c, dx, dy: srcB[c, dx, y0 + dy : y0 + dy + 8, :], -4)
        for c in range(4):
            resB[c, y0 : y0 + 8] = totals[c]

    def plane(x, carry):
        for half in range(r // 8):
            y0 = 8 * half
            totals = advect_tile(code[x, y0 : y0 + 8], lambda c, dx, dy: srcA[c, x + dx, y0 + dy : y0 + dy + 8, :], 0)
            for c in range(4):
                u[c, x, y0 : y0 + 8] = totals[c]
        return carry

    lax.fori_loop(0, p, plane, 0)
    for c in range(4):
        for x in range(p):
            u[c, x] = jnp.where(lane16 >= 120, roll(resB[c], -(16 * x + 12), 1), u[c, x])
    new_den[...] = u[3]

    vel_u = u.at[0:3]
    exchange_xy(sizes, me, vel_u, stripB, rxB, ryB, rcB, (sxyB, rxyB), extU)
    pack_z(extU, packU)
    exchange_z(sizes, me, packU, gotU, (szB, rzB))
    for c in range(3):
        both = jnp.where((lane & 7) < 4, gotU[0, c], gotU[1, c])
        for x in range(p + 8):
            wide[c, x, :, 0:128] = extU[c, x]
            wide[c, x, :, 128:256] = roll(both, -(8 * x + 4), 1)

    def yz_mask(nrows, first_row, block_rows, cells):
        row = lax.broadcasted_iota(jnp.int32, (nrows, 256), 0) - first_row + me[1] * block_rows
        spot = lanes((nrows, 256))
        z = jnp.where(spot < 192, spot, spot - 256) + me[2] * cells
        return (row >= 0) & (row < sizes[1] * block_rows) & (z >= 0) & (z < sizes[2] * cells)

    def x_ok(x, first, block):
        g = x - first + me[0] * block
        return (g >= 0) & (g < sizes[0] * block)

    mask0 = yz_mask(rows, HALO, r, 128)

    def around(ref, x, step):
        v = ref[x]
        total = ref[x + 1] + ref[x - 1]
        total = total + roll(v, -1, 0) + roll(v, 1, 0)
        total = total + roll(v, -step, 1) + roll(v, step, 1)
        return 6.0 * v - total

    def second(ref, x, scale, step):
        v = ref[x]
        first = (RELAX * scale) * v
        return first + RELAX * (scale * v - (RELAX * scale) * around(ref, x, step))

    def source0(x, carry):
        part = wide[0, x + 1] - wide[0, x - 1]
        v = wide[1, x]
        part = part + (roll(v, -1, 0) - roll(v, 1, 0))
        v = wide[2, x]
        part = part + (roll(v, -1, 1) - roll(v, 1, 1))
        s0[x] = jnp.where(mask0 & x_ok(x, HALO, p), -0.5 * part, 0.0)
        return carry

    lax.fori_loop(1, p + 7, source0, 0)

    def second0(x, carry):
        q0[x] = jnp.where(mask0 & x_ok(x, HALO, p), second(s0, x, 1.0, 1), 0.0)
        return carry

    lax.fori_loop(2, p + 6, second0, 0)

    def residual0(x, carry):
        r0[x] = (s0[x] - around(q0, x, 1))[:, 0:128]
        return carry

    lax.fori_loop(HALO, HALO + p, residual0, 0)
    lane8 = lanes((r // 2, 128))
    for x in range(p // 2):
        tmp0[...] = r0[HALO + 2 * x] + r0[HALO + 2 * x + 1]
        v = tmp0[pl.ds(HALO, r // 2, stride=2), :] + tmp0[pl.ds(HALO + 1, r // 2, stride=2), :]
        v = v + jnp.where((lane8 & 1) == 0, roll(v, -1, 1), roll(v, 1, 1))
        own1[0, x] = 0.125 * v

    p1, r1n = p // 2, r // 2
    exchange_xy(sizes, me, own1, strip1, rx1, ry1, rc1, (sxy1, rxy1), ext1)
    exchange_z(sizes, me, ext1, got1, (sz1, rz1))
    rows1 = r1n + 8
    lane1 = lanes((rows1, 128))
    for x in range(p1 + 8):
        wide1[x, :, 0:128] = ext1[0, x]
        wide1[x, :, 128:256] = jnp.where(lane1 < 64, got1[1, 0, x], got1[0, 0, x])
    mask1 = yz_mask(rows1, HALO, r1n, 128)
    for x in range(HALO - 1, HALO + p1 + 1):
        q1[x] = jnp.where(mask1 & x_ok(x, HALO, p1), second(wide1, x, 4.0, 2), 0.0)
    for x in range(HALO, HALO + p1):
        r1[x] = (wide1[x] - 0.25 * around(q1, x, 2))[:, 0:128]
    p2, r2n = p1 // 2, r1n // 2
    lane4 = lanes((r2n, 128))
    for x in range(p2):
        tmp1[...] = r1[HALO + 2 * x] + r1[HALO + 2 * x + 1]
        v = tmp1[pl.ds(HALO, r2n, stride=2), :] + tmp1[pl.ds(HALO + 1, r2n, stride=2), :]
        v = v + jnp.where((lane4 & 3) < 2, roll(v, -2, 1), roll(v, 2, 1))
        own2[x] = 0.125 * v

    comm = Comm(sizes, me, sxy2, rxy2)
    for slot, (dx, dy) in enumerate(FAR):
        comm.add((dx, dy, 0), own2, got2.at[2 - dx, 1 - dy], slot)
    for dx, dy in FAR:
        zero_if_missing(sizes, me, (dx, dy, 0), got2.at[dx + 2, dy + 1])
    got2[2, 1] = own2[...]
    ext2[...] = jnp.zeros(ext2.shape, jnp.float32)
    comm.wait()
    for a in range(5):
        for b in range(3):
            ext2[p2 * a : p2 * a + p2, r2n * b : r2n * b + r2n, :] = got2[a, b]
    exchange_z(sizes, me, ext2, gotz2, (sz2, rz2))
    lane2 = lanes((16, 128))
    mask2 = yz_mask(16, r2n, r2n, 128)
    planes2 = {}
    for x in range(2 * p2 - 2, 3 * p2 + 2):
        planes2[x] = jnp.concatenate([ext2[x], jnp.where(lane2 < 64, gotz2[1, x], gotz2[0, x])], axis=1)
    sum1[...] = jnp.zeros(sum1.shape, jnp.float32)
    for x in range(2 * p2 - 1, 3 * p2 + 1):
        v = jnp.where(mask2 & x_ok(x, 2 * p2, p2), second(planes2, x, 16.0, 4), 0.0)
        first_row = r2n - 1
        take = r2n + 2
        base = HALO - 2
        for side in range(2):
            part = v[first_row : first_row + take, 128 * side : 128 * side + 128]
            sum1[x, side, pl.ds(base, take, stride=2), :] = part
            sum1[x, side, pl.ds(base + 1, take, stride=2), :] = part
    for x1 in range(HALO - 1, HALO + p1 + 1):
        x2 = (x1 - HALO) // 2 + 2 * p2
        for side in range(2):
            v = q1[x1, :, 128 * side : 128 * side + 128] + sum1[x2, side]
            part = v[HALO - 2 : HALO - 2 + r1n + 4]
            fine[x1, side, pl.ds(0, r1n + 4, stride=2), :] = part
            fine[x1, side, pl.ds(1, r1n + 4, stride=2), :] = part
    for x in range(HALO - 1, HALO + p + 1):
        x1 = (x - HALO) // 2 + HALO
        coarse = jnp.concatenate([fine[x1, 0], fine[x1, 1]], axis=1)
        s0[x] = jnp.where(mask0 & x_ok(x, HALO, p), q0[x] + coarse, 0.0)
    for x in range(p):
        v = s0[x + HALO]
        cut = lambda t: t[HALO : HALO + r, 0:128]
        press[x] = cut(v)
        new_vel[0, x] = u[0, x] - 0.5 * cut(s0[x + HALO + 1] - s0[x + HALO - 1])
        new_vel[1, x] = u[1, x] - 0.5 * cut(roll(v, -1, 0) - roll(v, 1, 0))
        new_vel[2, x] = u[2, x] - 0.5 * cut(roll(v, -1, 1) - roll(v, 1, 1))


def step(sizes, velocity, density, offsets, eighths):
    p, r, _ = density.shape
    f32 = jnp.float32

    def vm(*shape):
        return pltpu.VMEM(shape, f32)

    def xy(f, p, r):
        return [vm(2, f, p, 4, 128), vm(2, f, 4, r, 128), vm(2, f, p, 4, 128), vm(2, 2, f, 4, 4, 128)]

    p1, r1, p2, r2 = p // 2, r // 2, p // 4, r // 4
    rows, rows1 = r + 8, r1 + 8
    dma = lambda n: pltpu.SemaphoreType.DMA((n,))
    scratch = (
        [vm(4, p, r, 128)] + xy(4, p, r)
        + [vm(4, p + 8, rows, 128), vm(4, rows, 128), vm(2, 4, rows, 128), vm(4, p + 8, rows, 128),
           vm(4, 9, rows, 128), pltpu.VMEM((p, r, 128), jnp.int32), pltpu.VMEM((r, 128), jnp.int32),
           vm(4, r, 128), vm(4, p, r, 128)]
        + xy(3, p, r)
        + [vm(3, p + 8, rows, 128), vm(3, rows, 128), vm(2, 3, rows, 128), vm(3, p + 8, rows, 256),
           vm(p + 8, rows, 256), vm(p + 8, rows, 256), vm(p + 8, rows, 128), vm(rows, 128), vm(1, p1, r1, 128)]
        + xy(1, p1, r1)
        + [vm(1, p1 + 8, rows1, 128), vm(2, 1, p1 + 8, rows1, 128), vm(p1 + 8, rows1, 256), vm(p1 + 8, rows1, 256),
           vm(p1 + 8, rows1, 128), vm(rows1, 128), vm(p2, r2, 128), vm(5, 3, p2, r2, 128), vm(5 * p2, 16, 128),
           vm(2, 5 * p2, 16, 128), vm(5 * p2, 2, rows1, 128), vm(p1 + 8, 2, rows, 128)]
        + [dma(8), dma(8), dma(2), dma(2)] * 3 + [dma(14), dma(14), dma(2), dma(2)]
    )
    vmem = pl.BlockSpec(memory_space=pltpu.VMEM)
    return pl.pallas_call(
        functools.partial(kernel, sizes),
        out_shape=(
            jax.ShapeDtypeStruct(velocity.shape, f32),
            jax.ShapeDtypeStruct(density.shape, f32),
            jax.ShapeDtypeStruct(density.shape, f32),
        ),
        in_specs=[vmem] * 4,
        out_specs=(vmem,) * 3,
        scratch_shapes=scratch,
        compiler_params=pltpu.CompilerParams(
            collective_id=0, has_side_effects=True, vmem_limit_bytes=48 * 1024 * 1024
        ),
    )(velocity, density, offsets, eighths)


def solution(mesh):
    sizes = tuple(mesh.shape[a] for a in ("gx", "gy", "gz"))
    block = P("gx", "gy", "gz")
    stacked = P(None, "gx", "gy", "gz")
    return jax.shard_map(
        functools.partial(step, sizes),
        mesh=mesh,
        in_specs=(stacked, block, stacked, stacked),
        out_specs=(stacked, block, block),
        check_vma=False,
    )
```

time: 278 us -> 62.9 us (0.23)
  the two profiles are of different devices: /device:TPU:21 before, /device:TPU:0 now
where the time goes in v1:
time: 62.9 us; the launch traced here: 62.6 us
  Pallas kernels  56.4 us (90%)
  local copies, waits for them, and re-layouts  5.55 us (9%)
  between operations  0.65 us (1%)
    pallas_call x1, Pallas kernels, step(): pl.pallas_call(functools.partial(kernel, sizes), out_shape=(jax.ShapeDtyp...  56.4 us
    unnamed x11, local copies, waits for them, and re-layouts  5.55 us

profile of v1, /device:TPU:0, one launch (start us, length us, event | category | flops | bytes accessed | tf_op | source)
XLA Modules:
  0.0 62.6 jit_solution(13392493298056361359)
XLA Ops:
  0.6 0.0 copy-start
  0.6 0.9 %copy-done = f32[3,8,16,128]{3,2,1,0:T(8,128)S(1)} copy-done((f32[3,8,16,128]{3,2,1,0:T(8,128)S(1)}, f32[3,8,16,128]{3,2,1,0:T(8,128)}, u32[]{:S(2)}) %copy-start) | copy-done | bytes 196632
  1.6 0.0 copy-start.1
  1.6 0.9 %copy-done.1 = s32[3,8,16,128]{3,2,1,0:T(8,128)S(1)} copy-done((s32[3,8,16,128]{3,2,1,0:T(8,128)S(1)}, s32[3,8,16,128]{3,2,1,0:T(8,128)}, u32[]{:S(2)}) %copy-start.1) | copy-done | bytes 196632
  2.5 0.0 copy-start.2
  2.5 0.9 %copy-done.2 = s32[3,8,16,128]{3,2,1,0:T(8,128)S(1)} copy-done((s32[3,8,16,128]{3,2,1,0:T(8,128)S(1)}, s32[3,8,16,128]{3,2,1,0:T(8,128)}, u32[]{:S(2)}) %copy-start.2) | copy-done | bytes 196632
  3.4 0.0 copy-start.3
  3.4 0.8 %copy-done.3 = f32[8,16,128]{2,1,0:T(8,128)S(1)} copy-done((f32[8,16,128]{2,1,0:T(8,128)S(1)}, f32[8,16,128]{2,1,0:T(8,128)}, u32[]{:S(2)}) %copy-start.3) | copy-done | bytes 65560
  4.3 56.4 %shard_map.67 = (f32[3,8,16,128]{3,2,1,0:T(8,128)S(1)}, f32[8,16,128]{2,1,0:T(8,128)S(1)}, f32[8,16,128]{2,1,0:T(8,128)S(1)}) custom-call(f32[3,8,16,128]{3,2,1,0:T(8,128)S(1)} %copy-done, f32[8,16,128]{2,1,0:T(8,128)S(1)} %copy-done.3, s32[3,8,16,128]{3,2,1,0:T(8,128)S(1)} %copy-done.1, s32[3,8,16,128]{3,2,1,0:T(8,128)S(1)} %copy-done.2), custom_call_target="tpu_custom_call" | custom-call | tf_op jit(solution)/shard_map/pallas_call | solution.py:380
  60.7 0.7 %copy.10 = f32[3,8,16,128]{3,2,1,0:T(8,128)} copy(f32[3,8,16,128]{3,2,1,0:T(8,128)S(1)} %get-tuple-element.6) | data formatting | bytes 393216
  61.4 0.6 %copy.11 = f32[8,16,128]{2,1,0:T(8,128)} copy(f32[8,16,128]{2,1,0:T(8,128)S(1)} %get-tuple-element.7) | data formatting | bytes 131072
  62.0 0.6 %copy.12 = f32[8,16,128]{2,1,0:T(8,128)} copy(f32[8,16,128]{2,1,0:T(8,128)S(1)} %get-tuple-element.8) | data formatting | bytes 131072
Async XLA Ops:
  0.6 0.9 %copy-start = (f32[3,8,16,128]{3,2,1,0:T(8,128)S(1)}, f32[3,8,16,128]{3,2,1,0:T(8,128)}, u32[]{:S(2)}) copy-start(f32[3,8,16,128]{3,2,1,0:T(8,128)} %vel.1) | copy-start | bytes 589828
  1.6 0.9 %copy-start.1 = (s32[3,8,16,128]{3,2,1,0:T(8,128)S(1)}, s32[3,8,16,128]{3,2,1,0:T(8,128)}, u32[]{:S(2)}) copy-start(s32[3,8,16,128]{3,2,1,0:T(8,128)} %off.1) | copy-start | bytes 589828
  2.5 0.9 %copy-start.2 = (s32[3,8,16,128]{3,2,1,0:T(8,128)S(1)}, s32[3,8,16,128]{3,2,1,0:T(8,128)}, u32[]{:S(2)}) copy-start(s32[3,8,16,128]{3,2,1,0:T(8,128)} %eig.1) | copy-start | bytes 589828
  3.4 0.8 %copy-start.3 = (f32[8,16,128]{2,1,0:T(8,128)S(1)}, f32[8,16,128]{2,1,0:T(8,128)}, u32[]{:S(2)}) copy-start(f32[8,16,128]{2,1,0:T(8,128)} %den.1) | copy-start | bytes 196612

commit v2 on v1

--- a/solution.py
+++ b/solution.py
@@ -65,7 +65,7 @@
     return {-1: 0, 1: 1}[d]
 
 
-def exchange_xy(sizes, me, own, strips, rx, ry, rc, sems, out, zero=True):
+def exchange_xy(sizes, me, own, strips, rx, ry, rc, sems, out, meanwhile=None):
     f, p, r, _ = own.shape
     for i in range(p):
         strips[0, :, i] = own[:, i, 0:HALO, :]
@@ -84,6 +84,8 @@
         ref = rx.at[pick_x(dx)] if dy == 0 else ry.at[pick_x(dy)] if dx == 0 else rc.at[pick_x(dx), pick_x(dy)]
         zero_if_missing(sizes, me, (dx, dy, 0), ref)
     out[:, HALO : HALO + p, HALO : HALO + r, :] = own[...]
+    if meanwhile is not None:
+        meanwhile()
     comm.wait()
     for sx, xs in ((0, slice(0, HALO)), (1, slice(HALO + p, HALO + p + HALO))):
         out[:, xs, HALO : HALO + r, :] = rx[sx]
@@ -144,12 +146,15 @@
     return totals
 
 
-def kernel(sizes, vel, den, off, eig, new_vel, new_den, press, fields, stripA, rxA, ryA, rcA, ext, packed,
+def kernel(sizes, vel, den, off_hbm, eig_hbm, new_vel, new_den, press, off, eig, fetch_sem, fields, stripA, rxA, ryA, rcA, ext, packed,
            gotP, srcA, srcB, code, codeB, resB, u, stripB, rxB, ryB, rcB, extU, packU, gotU, wide, s0, q0, r0,
            tmp0, own1, strip1, rx1, ry1, rc1, ext1, got1, wide1, q1, r1, tmp1, own2, got2, ext2, gotz2, sum1, fine,
            sxyA, rxyA, szA, rzA, sxyB, rxyB, szB, rzB, sxy1, rxy1, sz1, rz1, sxy2, rxy2, sz2, rz2):
     me = tuple(lax.axis_index(a) for a in ("gx", "gy", "gz"))
     p, r = den.shape[0], den.shape[1]
+    fetch = [pltpu.make_async_copy(off_hbm, off, fetch_sem.at[0]), pltpu.make_async_copy(eig_hbm, eig, fetch_sem.at[1])]
+    for copy in fetch:
+        copy.start()
     fields[0:3] = vel[...]
     fields[3] = den[...]
 
@@ -166,19 +171,23 @@
         count = count + jnp.where(ok, 1, 0)
     pl.semaphore_wait(barrier, count)
 
-    whole = (off[0] + 4) + 8 * (off[1] + 4) + 64 * (off[2] + 4)
-    code[...] = whole + 512 * eig[0] + 4096 * eig[1] + 32768 * eig[2]
-    lane16 = lanes((r, 128))
-    total = roll(code[0], 12, 1)
-    for g in range(1, p):
-        total = jnp.where(lane16 >= 16 * g, roll(code[g], 16 * g + 12, 1), total)
-    codeB[...] = total
-
-    exchange_xy(sizes, me, fields, stripA, rxA, ryA, rcA, (sxyA, rxyA), ext)
+    def positions():
+        for copy in fetch:
+            copy.wait()
+        whole = (off[0] + 4) + 8 * (off[1] + 4) + 64 * (off[2] + 4)
+        code[...] = whole + 512 * eig[0] + 4096 * eig[1] + 32768 * eig[2]
+        lane16 = lanes((r, 128))
+        total = roll(code[0], 12, 1)
+        for g in range(1, p):
+            total = jnp.where(lane16 >= 16 * g, roll(code[g], 16 * g + 12, 1), total)
+        codeB[...] = total
+
+    exchange_xy(sizes, me, fields, stripA, rxA, ryA, rcA, (sxyA, rxyA), ext, positions)
     pack_z(ext, packed)
     exchange_z(sizes, me, packed, gotP, (szA, rzA))
 
     rows = r + 8
+    lane16 = lanes((r, 128))
     lane = lanes((rows, 128))
     for c in range(4):
         below, above = gotP[0, c], gotP[1, c]
@@ -204,15 +213,16 @@
         for c in range(4):
             resB[c, y0 : y0 + 8] = totals[c]
 
-    def plane(x, carry):
-        for half in range(r // 8):
-            y0 = 8 * half
+    for half in range(r // 8):
+        y0 = 8 * half
+
+        def plane(x, carry, y0=y0):
             totals = advect_tile(code[x, y0 : y0 + 8], lambda c, dx, dy: srcA[c, x + dx, y0 + dy : y0 + dy + 8, :], 0)
             for c in range(4):
                 u[c, x, y0 : y0 + 8] = totals[c]
-        return carry
-
-    lax.fori_loop(0, p, plane, 0)
+            return carry
+
+        lax.fori_loop(0, p, plane, 0)
     for c in range(4):
         for x in range(p):
             u[c, x] = jnp.where(lane16 >= 120, roll(resB[c], -(16 * x + 12), 1), u[c, x])
@@ -363,7 +373,7 @@
     rows, rows1 = r + 8, r1 + 8
     dma = lambda n: pltpu.SemaphoreType.DMA((n,))
     scratch = (
-        [vm(4, p, r, 128)] + xy(4, p, r)
+        [pltpu.VMEM(offsets.shape, jnp.int32), pltpu.VMEM(eighths.shape, jnp.int32), dma(2), vm(4, p, r, 128)] + xy(4, p, r)
         + [vm(4, p + 8, rows, 128), vm(4, rows, 128), vm(2, 4, rows, 128), vm(4, p + 8, rows, 128),
            vm(4, 9, rows, 128), pltpu.VMEM((p, r, 128), jnp.int32), pltpu.VMEM((r, 128), jnp.int32),
            vm(4, r, 128), vm(4, p, r, 128)]
@@ -384,7 +394,7 @@
             jax.ShapeDtypeStruct(density.shape, f32),
             jax.ShapeDtypeStruct(density.shape, f32),
         ),
-        in_specs=[vmem] * 4,
+        in_specs=[vmem] * 2 + [pl.BlockSpec(memory_space=pltpu.HBM)] * 2,
         out_specs=(vmem,) * 3,
         scratch_shapes=scratch,
         compiler_params=pltpu.CompilerParams(

time: 62.9 us -> 58.5 us (0.930)
  Pallas kernels: 56.4 us -> 52 us
    pallas_call x1, Pallas kernels: 56.4 us -> 52 us  [step(): pl.pallas_call(functools.partial(kernel, sizes), out_shape=(jax.ShapeDtyp...]
where the time goes in v2:
time: 58.5 us; the launch traced here: 58.2 us
  Pallas kernels  52 us (89%)
  local copies, waits for them, and re-layouts  5.55 us (9%)
  between operations  0.65 us (1%)
    pallas_call x1, Pallas kernels, step(): pl.pallas_call(functools.partial(kernel, sizes), out_shape=(jax.ShapeDtyp...  52 us
    unnamed x11, local copies, waits for them, and re-layouts  5.55 us

profile of v2, /device:TPU:0, one launch (start us, length us, event | category | flops | bytes accessed | tf_op | source)
XLA Modules:
  0.0 58.2 jit_solution(7556223457951822451)
XLA Ops:
  0.6 0.0 copy-start
  0.6 0.9 %copy-done = f32[3,8,16,128]{3,2,1,0:T(8,128)S(1)} copy-done((f32[3,8,16,128]{3,2,1,0:T(8,128)S(1)}, f32[3,8,16,128]{3,2,1,0:T(8,128)}, u32[]{:S(2)}) %copy-start) | copy-done | bytes 196632
  1.6 0.0 copy-start.1
  1.6 0.9 %copy-done.1 = s32[3,8,16,128]{3,2,1,0:T(8,128)S(1)} copy-done((s32[3,8,16,128]{3,2,1,0:T(8,128)S(1)}, s32[3,8,16,128]{3,2,1,0:T(8,128)}, u32[]{:S(2)}) %copy-start.1) | copy-done | bytes 196632
  2.5 0.0 copy-start.2
  2.5 0.9 %copy-done.2 = s32[3,8,16,128]{3,2,1,0:T(8,128)S(1)} copy-done((s32[3,8,16,128]{3,2,1,0:T(8,128)S(1)}, s32[3,8,16,128]{3,2,1,0:T(8,128)}, u32[]{:S(2)}) %copy-start.2) | copy-done | bytes 196632
  3.4 0.0 copy-start.3
  3.4 0.8 %copy-done.3 = f32[8,16,128]{2,1,0:T(8,128)S(1)} copy-done((f32[8,16,128]{2,1,0:T(8,128)S(1)}, f32[8,16,128]{2,1,0:T(8,128)}, u32[]{:S(2)}) %copy-start.3) | copy-done | bytes 65560
  4.3 52.0 %shard_map.67 = (f32[3,8,16,128]{3,2,1,0:T(8,128)S(1)}, f32[8,16,128]{2,1,0:T(8,128)S(1)}, f32[8,16,128]{2,1,0:T(8,128)S(1)}) custom-call(f32[3,8,16,128]{3,2,1,0:T(8,128)S(1)} %copy-done, f32[8,16,128]{2,1,0:T(8,128)S(1)} %copy-done.3, s32[3,8,16,128]{3,2,1,0:T(8,128)S(1)} %copy-done.1, s32[3,8,16,128]{3,2,1,0:T(8,128)S(1)} %copy-done.2), custom_call_target="tpu_custom_call" | custom-call | tf_op jit(solution)/shard_map/pallas_call | solution.py:390
  56.3 0.7 %copy.10 = f32[3,8,16,128]{3,2,1,0:T(8,128)} copy(f32[3,8,16,128]{3,2,1,0:T(8,128)S(1)} %get-tuple-element.6) | data formatting | bytes 393216
  57.0 0.6 %copy.11 = f32[8,16,128]{2,1,0:T(8,128)} copy(f32[8,16,128]{2,1,0:T(8,128)S(1)} %get-tuple-element.7) | data formatting | bytes 131072
  57.6 0.6 %copy.12 = f32[8,16,128]{2,1,0:T(8,128)} copy(f32[8,16,128]{2,1,0:T(8,128)S(1)} %get-tuple-element.8) | data formatting | bytes 131072
Async XLA Ops:
  0.6 0.9 %copy-start = (f32[3,8,16,128]{3,2,1,0:T(8,128)S(1)}, f32[3,8,16,128]{3,2,1,0:T(8,128)}, u32[]{:S(2)}) copy-start(f32[3,8,16,128]{3,2,1,0:T(8,128)} %vel.1) | copy-start | bytes 589828
  1.6 0.9 %copy-start.1 = (s32[3,8,16,128]{3,2,1,0:T(8,128)S(1)}, s32[3,8,16,128]{3,2,1,0:T(8,128)}, u32[]{:S(2)}) copy-start(s32[3,8,16,128]{3,2,1,0:T(8,128)} %off_hbm.1) | copy-start | bytes 589828
  2.5 0.9 %copy-start.2 = (s32[3,8,16,128]{3,2,1,0:T(8,128)S(1)}, s32[3,8,16,128]{3,2,1,0:T(8,128)}, u32[]{:S(2)}) copy-start(s32[3,8,16,128]{3,2,1,0:T(8,128)} %eig_hbm.1) | copy-start | bytes 589828
  3.4 0.8 %copy-start.3 = (f32[8,16,128]{2,1,0:T(8,128)S(1)}, f32[8,16,128]{2,1,0:T(8,128)}, u32[]{:S(2)}) copy-start(f32[8,16,128]{2,1,0:T(8,128)} %den.1) | copy-start | bytes 196612
